TPU v7x, 32 devices: a whole 2x2x4 slice. The times are simulated.
32 devices in a mesh: shard: 8 (over z, y), model: 4 (over x, core).
Axes of the slice: x: 2, y: 2, z: 4, core: 2. Of those that a mesh axis runs over, the one named last changes fastest.
Arguments:
- gradients: float32 [32, 128, 4096], P(None, 'shard', 'model'), may hold values from -6 to 6
- momentum: float32 [32, 128, 4096], P(None, 'shard', 'model'), may hold values from -6 to 6
- weights: float32 [32, 128, 4096], P(None, 'shard', 'model'), may hold values from -0.1875 to 0.1875
Outputs:
- new_weights: float32 [32, 128, 4096], P(None, 'shard', 'model')
- new_momentum: float32 [32, 128, 4096], P(None, 'shard', 'model')
All inputs are finite; a program needn't handle non-finite values.
Results may differ from a plain program's by a relative error of at most 0.00015.
Values sent between devices are 32-bit elements; how exact they have to be, the bound alone decides.
A program may use at most 128 MiB of HBM per device.

v0:
```python
import jax
import jax.numpy as jnp
from jax import lax
from jax.sharding import PartitionSpec as P

ITERS = 4


hold_rate = 0.8
learn_rate = 1.0


def on_device(gradients, momentum, weights):
    new_momentum = hold_rate * momentum + gradients
    moved = lax.all_to_all(new_momentum, "shard", split_axis=0, concat_axis=1, tiled=True)
    whole = lax.all_to_all(moved, "model", split_axis=0, concat_axis=2, tiled=True)
    iterate = whole * lax.rsqrt(jnp.sum(whole * whole, axis=(1, 2), keepdims=True) + 1e-06)
    for step in range(ITERS):
        gram = jnp.einsum("mik,mjk->mij", iterate, iterate, precision=lax.Precision.HIGHEST)
        mixed = -4.775 * gram + 2.0315 * jnp.einsum(
            "mij,mjk->mik", gram, gram, precision=lax.Precision.HIGHEST
        )
        iterate = 3.4445 * iterate + jnp.einsum(
            "mij,mjk->mik", mixed, iterate, precision=lax.Precision.HIGHEST
        )
    iterate = lax.all_to_all(iterate, "model", split_axis=2, concat_axis=0, tiled=True)
    back = lax.all_to_all(iterate, "shard", split_axis=1, concat_axis=0, tiled=True)
    new_weights = weights - learn_rate * back
    return (new_weights, new_momentum)


def solution(mesh):
    placed = (P(None, "shard", "model"), P(None, "shard", "model"), P(None, "shard", "model"))
    return jax.shard_map(
        on_device,
        mesh=mesh,
        in_specs=placed,
        out_specs=(P(None, "shard", "model"), P(None, "shard", "model")),
        check_vma=False,
    )
```

profile of v0, /device:TPU:0, one launch (start us, length us, event | category | flops | bytes accessed | tf_op | source)
XLA Modules:
  0.0 208.4 jit_solution(6684310043670269516)
XLA Ops:
  0.6 2.7 %multiply_add_fusion = f32[32,16,1024]{2,1,0:T(8,128)S(1)} fusion(f32[32,16,1024]{2,1,0:T(8,128)} %param.3, f32[32,16,1024]{2,1,0:T(8,128)} %param.4), kind=kLoop, calls=%fused_computation.10 | loop fusion | flops 1048576 | bytes 6291456 | tf_op jit(solution)/shard_map/add | solution.py:14
  3.3 0.0 copy-start
  3.3 55.3 %all_to_all.63 = f32[32,16,1024]{2,1,0:T(8,128)S(1)} all-to-all(f32[32,16,1024]{2,1,0:T(8,128)S(1)} %multiply_add_fusion), channel_id=1, replica_groups=mesh['shard'=8,'model'=4] {'shard'}, dimensions={0} | all-to-all | bytes 4194304 | tf_op jit(solution)/shard_map/all_to_all | solution.py:15
  58.6 0.0 copy-done
  58.6 0.2 copy.30
  58.9 28.2 %all_to_all.64 = f32[4,128,1024]{2,1,0:T(8,128)S(1)} all-to-all(f32[4,128,1024]{2,1,0:T(8,128)S(1)} %bitcast.57), channel_id=1, replica_groups=mesh['shard'=8,'model'=4] {'model'}, dimensions={0} | all-to-all | bytes 4194304 | tf_op jit(solution)/shard_map/all_to_all | solution.py:16
  87.1 1.1 multiply_reduce_fusion
  88.9 1.8 fusion.4
  90.7 0.2 fusion.10
  91.0 2.6 %multiply_bitcast_fusion.1 = (f32[1,128,4,1024]{3,1,2,0:T(8,128)}, f32[1,128,4,1024]{3,1,2,0:T(8,128)}) fusion(f32[4,128,1024]{2,1,0:T(8,128)S(1)} %all_to_all.64, f32[]{:T(128)S(6)} %rsqrt.4), kind=kLoop, calls=%fused_computation.12 | loop fusion | flops 1048576 | bytes 6291460 | tf_op jit(solution)/shard_map/mul | solution.py:17
  93.5 1.9 copy.32
  95.4 2.9 %copy.31 = f32[1,128,4,1024]{1,3,2,0:T(8,128)} copy(f32[1,128,4,1024]{3,1,2,0:T(8,128)} %get-tuple-element.3) | data formatting | bytes 4194304 | tf_op jit(solution)/shard_map/mul | solution.py:23
  98.3 3.0 %copy.33 = f32[128,4096]{1,0:T(8,128)} copy(f32[128,4096]{0,1:T(8,128)} %bitcast.58) | data formatting | bytes 4194304 | tf_op jit(solution)/shard_map/mul | solution.py:23
  101.3 3.6 %convolution_add_fusion.3 = f32[128,4096]{1,0:T(8,128)S(1)} fusion(f32[128,4096]{1,0:T(8,128)} %copy.33, f32[128,128]{1,0:T(8,128)S(1)} %fusion.10, f32[128,4096]{0,1:T(8,128)S(1)} %bitcast.56), kind=kOutput, calls=%fused_computation.4 | convolution fusion | flops 805830656 | bytes 6356992 | tf_op jit(solution)/shard_map/mij,mjk->mik/dot_general | solution.py:23
  104.9 1.8 fusion.12
  106.7 0.2 fusion.9
  106.9 2.0 convolution_add_fusion.2
  108.9 1.8 fusion.13
  110.7 0.2 fusion.8
  110.9 2.0 convolution_add_fusion.1
  113.0 1.8 fusion.14
  114.8 0.2 fusion.7
  115.0 2.3 %fusion = f32[1,128,4096]{2,1,0:T(8,128)S(1)} fusion(f32[128,128]{1,0:T(8,128)S(1)} %fusion.7, f32[128,4096]{1,0:T(8,128)S(1)} %convolution_add_fusion.1), kind=kOutput, calls=%fused_computation.1 | convolution fusion | flops 806354944 | bytes 4259840 | tf_op jit(solution)/shard_map/mij,mjk->mik/dot_general | solution.py:23
  117.3 3.7 %copy.34 = f32[1,128,4096]{1,0,2:T(1,128)} copy(f32[1,128,4096]{2,1,0:T(8,128)S(1)} %fusion) | data formatting | bytes 4194304 | tf_op jit(solution)/shard_map/add | solution.py:23
  121.0 29.2 %all_to_all.65 = f32[1,128,4096]{1,0,2:T(1,128)S(1)} all-to-all(f32[1,128,4096]{1,0,2:T(1,128)} %copy.34), channel_id=1, replica_groups=mesh['shard'=8,'model'=4] {'model'}, dimensions={2} | all-to-all | bytes 4194304 | tf_op jit(solution)/shard_map/all_to_all | solution.py:26
  150.2 2.0 copy.35
  152.2 51.7 %all_to_all.66 = f32[4,128,1024]{2,0,1:T(4,128)S(1)} all-to-all(f32[4,128,1024]{2,0,1:T(4,128)} %copy.35), channel_id=1, replica_groups=mesh['shard'=8,'model'=4] {'shard'}, dimensions={1} | all-to-all | bytes 4194304 | tf_op jit(solution)/shard_map/all_to_all | solution.py:27
  203.8 1.2 copy.36
  205.1 0.0 copy-start.1
  205.1 0.2 copy.37
  205.3 1.3 copy-done.1
  206.6 1.7 bitcast_subtract_fusion
Async XLA Ops:
  3.3 55.4 %copy-start = (f32[32,16,1024]{2,1,0:T(8,128)}, f32[32,16,1024]{2,1,0:T(8,128)S(1)}, u32[]{:S(2)}) copy-start(f32[32,16,1024]{2,1,0:T(8,128)S(1)} %multiply_add_fusion) | copy-start | bytes 6291460
  205.1 1.6 copy-start.1
where the time goes:
time: 209 us; the launch traced here: 208 us
  blocking collectives  164 us (78%)
  matrix products  17.9 us (9%)
  local copies, waits for them, and re-layouts  16.4 us (8%)
  other arithmetic  8.09 us (4%)
    all_to_all x1, blocking collectives, on_device(): lax.all_to_all(new_momentum, 'shard', split_axis=0, concat_axis=1, tiled=...  55.3 us
    all_to_all x1, blocking collectives, on_device(): lax.all_to_all(iterate, 'shard', split_axis=1, concat_axis=0, tiled=True)  51.7 us
    all_to_all x1, blocking collectives, on_device(): lax.all_to_all(iterate, 'model', split_axis=2, concat_axis=0, tiled=True)  29.2 us
    all_to_all x1, blocking collectives, on_device(): lax.all_to_all(moved, 'model', split_axis=0, concat_axis=2, tiled=True)  28.2 us
    dot_general x4, matrix products, on_device(): jnp.einsum('mij,mjk->mik', mixed, iterate, precision=lax.Precision.HIGHEST)  9.94 us
    dot_general x4, matrix products, on_device(): jnp.einsum('mik,mjk->mij', iterate, iterate, precision=lax.Precision.HIGH...  7.17 us
    mul x2, local copies, waits for them, and re-layouts, on_device(): 3.4445 * iterate  5.84 us

commit v1 on v0

v1 whole, which is shorter than its diff:
```python
import functools

import jax
import jax.numpy as jnp
from jax import lax
from jax.experimental import pallas as pl
from jax.experimental.pallas import tpu as pltpu
from jax.sharding import PartitionSpec as P

ITERS = 4
MESH = pl.DeviceIdType.MESH
HIGHEST = lax.Precision.HIGHEST


hold_rate = 0.8
learn_rate = 1.0


def mm(a, b):
    return jnp.dot(a, b, precision=HIGHEST, preferred_element_type=jnp.float32)


def direction(gram):
    side = gram.shape[-1]
    row = lax.broadcasted_iota(jnp.int32, (side, side), 0)
    col = lax.broadcasted_iota(jnp.int32, (side, side), 1)
    diagonal = row == col
    squares = jnp.sum(jnp.where(diagonal, gram, 0.0), axis=(0, 1), keepdims=True)
    scale = lax.rsqrt(squares + 1e-06)
    a = gram * scale * scale
    q = jnp.where(diagonal, jnp.broadcast_to(scale, gram.shape), 0.0)
    for step in range(ITERS):
        mixed = -4.775 * a + 2.0315 * mm(a, a)
        if step == 0:
            q_next = 3.4445 * q + mixed * scale
        else:
            q_next = 3.4445 * q + mm(mixed, q)
        if step < ITERS - 1:
            half = 3.4445 * a + mm(mixed, a)
            a = 3.4445 * half + mm(mixed, half)
        q = q_next
    return q


def offsets(n):
    return sorted(range(1, n), key=lambda off: -min(off, n - off))


def exchange_kernel(n, k, x_ref, back_ref, held, result, grams,
                    f_send, f_recv, g_send, g_recv, b_send, b_recv, own_in, own_out):
    me = lax.axis_index("shard")
    col = lax.axis_index("model")
    local, _, rows, wide = held.shape
    side = n * rows

    def peer(off):
        return lax.rem(me + off, n)

    def forward(j, off):
        to = peer(off)
        return pltpu.make_async_remote_copy(
            src_ref=x_ref.at[to * local + j], dst_ref=held.at[j, me],
            send_sem=f_send.at[j, off], recv_sem=f_recv.at[j, off],
            device_id={"shard": to}, device_id_type=MESH)

    def share(j, off):
        return pltpu.make_async_remote_copy(
            src_ref=grams.at[j, col], dst_ref=grams.at[j, col],
            send_sem=g_send.at[j, off], recv_sem=g_recv.at[j, off],
            device_id={"model": lax.rem(col + off, k)}, device_id_type=MESH)

    def backward(j, off):
        to = peer(off)
        return pltpu.make_async_remote_copy(
            src_ref=result.at[j, to], dst_ref=back_ref.at[me * local + j],
            send_sem=b_send.at[j, off], recv_sem=b_recv.at[j, off],
            device_id={"shard": to}, device_id_type=MESH)

    def mine_in(j):
        return pltpu.make_async_copy(x_ref.at[me * local + j], held.at[j, me], own_in.at[j])

    def mine_out(j):
        return pltpu.make_async_copy(result.at[j, me], back_ref.at[me * local + j], own_out.at[j])

    barrier = pltpu.get_barrier_semaphore()
    for off in range(1, n):
        pl.semaphore_signal(barrier, inc=1, device_id={"shard": peer(off)}, device_id_type=MESH)
    for off in range(1, k):
        pl.semaphore_signal(barrier, inc=1, device_id={"model": lax.rem(col + off, k)}, device_id_type=MESH)
    pl.semaphore_wait(barrier, n + k - 2)

    @pl.loop(0, local)
    def _(j):
        for off in offsets(n):
            forward(j, off).start()
        mine_in(j).start()

    @pl.loop(0, local)
    def _(j):
        for off in offsets(n):
            forward(j, off).wait_recv()
        mine_in(j).wait()
        x = held[j].reshape(side, wide)
        grams[j, col] = lax.dot_general(
            x, x, (((1,), (1,)), ((), ())), precision=HIGHEST, preferred_element_type=jnp.float32)
        for off in range(1, k):
            share(j, off).start()
        for off in range(1, k):
            share(j, off).wait_recv()
        gram = grams[j, 0]
        for i in range(1, k):
            gram = gram + grams[j, i]
        result[j] = mm(direction(gram), x).reshape(n, rows, wide)
        for off in offsets(n):
            backward(j, off).start()
        mine_out(j).start()

    @pl.loop(0, local)
    def _(j):
        for off in range(1, n):
            forward(j, off).wait_send()
            backward(j, off).wait()
        for off in range(1, k):
            share(j, off).wait_send()
        mine_out(j).wait()


def by_kernel(n, k, x):
    mats, rows, wide = x.shape
    local = mats // n
    side = n * rows
    dma = pltpu.SemaphoreType.DMA
    return pl.pallas_call(
        functools.partial(exchange_kernel, n, k),
        out_shape=jax.ShapeDtypeStruct(x.shape, jnp.float32),
        in_specs=[pl.BlockSpec(memory_space=pl.ANY)],
        out_specs=pl.BlockSpec(memory_space=pl.ANY),
        scratch_shapes=[
            pltpu.VMEM((local, n, rows, wide), jnp.float32),
            pltpu.VMEM((local, n, rows, wide), jnp.float32),
            pltpu.VMEM((local, k, side, side), jnp.float32),
            dma((local, n)), dma((local, n)),
            dma((local, k)), dma((local, k)),
            dma((local, n)), dma((local, n)),
            dma((local,)), dma((local,)),
        ],
        compiler_params=pltpu.CompilerParams(
            collective_id=0, has_side_effects=True, vmem_limit_bytes=32 * 1024 * 1024),
    )(x)


def on_device(n, k, gradients, momentum, weights):
    new_momentum = hold_rate * momentum + gradients
    back = by_kernel(n, k, new_momentum)
    new_weights = weights - learn_rate * back
    return (new_weights, new_momentum)


def solution(mesh):
    placed = P(None, "shard", "model")
    return jax.shard_map(
        functools.partial(on_device, mesh.shape["shard"], mesh.shape["model"]),
        mesh=mesh,
        in_specs=(placed, placed, placed),
        out_specs=(placed, placed),
        check_vma=False,
    )
```

time: 209 us -> 102 us (0.49)
  blocking collectives: 164 us -> 0 us
  Pallas kernels: 0 us -> 96.9 us
  matrix products: 17.9 us -> 0 us
  local copies, waits for them, and re-layouts: 16.4 us -> 0.01 us
  other arithmetic: 8.09 us -> 4.71 us
    all_to_all x4 -> x0, blocking collectives: 164 us -> none  [the longest x1 55.3 us: on_device(): lax.all_to_all(new_momentum, 'shard', split_axis=0, concat_axis=1, tiled=...]
    pallas_call x0 -> x1, Pallas kernels: none -> 96.9 us  [by_kernel(): pl.pallas_call(functools.partial(exchange_kernel, n, k), out_shape=jax.Sh...]
    dot_general x12 -> x0, matrix products: 17.9 us -> none  [the longest x4 9.94 us: on_device(): jnp.einsum('mij,mjk->mik', mixed, iterate, precision=lax.Precision.HIGHEST)]
    mul x3 -> x0, local copies, waits for them, and re-layouts: 7.74 us -> none  [the longest x2 5.84 us: on_device(): 3.4445 * iterate]
    add x1 -> x0, local copies, waits for them, and re-layouts: 3.7 us -> none  [on_device(): 3.4445 * iterate]
    all_to_all x4 -> x0, local copies, waits for them, and re-layouts: 3.65 us -> none  [the longest x1 1.96 us: on_device(): lax.all_to_all(iterate, 'model', split_axis=2, concat_axis=0, tiled=True)]
    mul x1 -> x0, other arithmetic: 2.56 us -> none  [on_device(): whole * lax.rsqrt(jnp.sum(whole * whole, axis=(1, 2), keepdims=True) + 1e...]
where the time goes in v1:
time: 102 us
  Pallas kernels  96.9 us (95%)
  other arithmetic  4.71 us (5%)
    pallas_call x1, Pallas kernels, by_kernel(): pl.pallas_call(functools.partial(exchange_kernel, n, k), out_shape=jax.Sh...  96.9 us
    add x1, other arithmetic, on_device(): new_momentum = hold_rate * momentum + gradients  2.83 us

profile of v1, /device:TPU:0, one launch (start us, length us, event | category | flops | bytes accessed | tf_op | source)
XLA Modules:
  0.0 102.3 jit_solution(12658191060856850005)
XLA Ops:
  0.6 2.8 %multiply_add_fusion.x_ref = f32[32,16,1024]{2,1,0:T(8,128)S(1)} fusion(f32[32,16,1024]{2,1,0:T(8,128)} %param.3, f32[32,16,1024]{2,1,0:T(8,128)} %param.4), kind=kLoop, calls=%fused_computation | loop fusion | flops 1048576 | bytes 6291456 | tf_op jit(solution)/shard_map/add | solution.py:153
  3.5 0.0 copy-start
  3.5 0.0 copy-start.1
  3.5 96.9 %shard_map.50 = f32[32,16,1024]{2,1,0:T(8,128)S(1)} custom-call(f32[32,16,1024]{2,1,0:T(8,128)S(1)} %multiply_add_fusion.x_ref), custom_call_target="tpu_custom_call" | custom-call | tf_op jit(solution)/shard_map/pallas_call | solution.py:133
  100.4 0.0 copy-done.1
  100.4 1.9 %sub.3 = f32[32,16,1024]{2,1,0:T(8,128)} subtract(f32[32,16,1024]{2,1,0:T(8,128)S(1)} %copy-done.1, f32[32,16,1024]{2,1,0:T(8,128)S(1)} %shard_map.50) | non-fusion elementwise | flops 524288 | bytes 6291456 | tf_op jit(solution)/shard_map/sub | solution.py:155
  102.3 0.0 copy-done
Async XLA Ops:
  3.5 98.8 %copy-start = (f32[32,16,1024]{2,1,0:T(8,128)}, f32[32,16,1024]{2,1,0:T(8,128)S(1)}, u32[]{:S(2)}) copy-start(f32[32,16,1024]{2,1,0:T(8,128)S(1)} %multiply_add_fusion.x_ref) | copy-start | bytes 6291460
  3.5 96.9 %copy-start.1 = (f32[32,16,1024]{2,1,0:T(8,128)S(1)}, f32[32,16,1024]{2,1,0:T(8,128)}, u32[]{:S(2)}) copy-start(f32[32,16,1024]{2,1,0:T(8,128)} %param.5) | copy-start | bytes 6291460

commit v2 on v1

v2 whole, which is shorter than its diff:
```python
import functools

import jax
import jax.numpy as jnp
from jax import lax
from jax.experimental import pallas as pl
from jax.experimental.pallas import tpu as pltpu
from jax.sharding import PartitionSpec as P

ITERS = 4
VMEM_LIMIT = 40 * 1024 * 1024
FINISH_LIMIT = 16 * 1024 * 1024
MESH = pl.DeviceIdType.MESH
HIGHEST = lax.Precision.HIGHEST


hold_rate = 0.8
learn_rate = 1.0


def mm(a, b):
    return jnp.dot(a, b, precision=HIGHEST, preferred_element_type=jnp.float32)


def direction(gram):
    side = gram.shape[-1]
    row = lax.broadcasted_iota(jnp.int32, (side, side), 0)
    col = lax.broadcasted_iota(jnp.int32, (side, side), 1)
    diagonal = row == col
    squares = jnp.sum(jnp.where(diagonal, gram, 0.0), axis=(0, 1), keepdims=True)
    scale = lax.rsqrt(squares + 1e-06)
    a = gram * scale * scale
    q = jnp.where(diagonal, jnp.broadcast_to(scale, gram.shape), 0.0)
    for step in range(ITERS):
        mixed = -4.775 * a + 2.0315 * mm(a, a)
        if step == 0:
            q_next = 3.4445 * q + mixed * scale
        else:
            q_next = 3.4445 * q + mm(mixed, q)
        if step < ITERS - 1:
            half = 3.4445 * a + mm(mixed, a)
            a = 3.4445 * half + mm(mixed, half)
        q = q_next
    return q


def partner(me, off, n):
    if n & (n - 1):
        return lax.rem(me + off, n)
    for bit in range(n.bit_length() - 1):
        if (off >> bit) & 1:
            me = me + (1 - 2 * ((me // (1 << bit)) % 2)) * (1 << bit)
    return me


def exchange_kernel(n, k, g_ref, m_ref, back_ref, new_ref, grad, moved, held, result, grams,
                    l_grad, l_moved, f_send, f_recv, g_send, g_recv, b_send, b_recv,
                    own_in, own_out, own_new):
    me = lax.axis_index("shard")
    col = lax.axis_index("model")
    local, _, rows, wide = held.shape
    side = n * rows

    def chunk(j):
        return pl.ds(j * n, n)

    def load_grad(j):
        return pltpu.make_async_copy(g_ref.at[chunk(j)], grad.at[j], l_grad.at[j])

    def load_moved(j):
        return pltpu.make_async_copy(m_ref.at[chunk(j)], moved.at[j], l_moved.at[j])

    def store_new(j):
        return pltpu.make_async_copy(moved.at[j], new_ref.at[chunk(j)], own_new.at[j])

    def forward(j, off):
        to = partner(me, off, n)
        return pltpu.make_async_remote_copy(
            src_ref=moved.at[j, to], dst_ref=held.at[j, me],
            send_sem=f_send.at[j, off], recv_sem=f_recv.at[j, off],
            device_id={"shard": to}, device_id_type=MESH)

    def share(j, off):
        return pltpu.make_async_remote_copy(
            src_ref=grams.at[j, col], dst_ref=grams.at[j, col],
            send_sem=g_send.at[j, off], recv_sem=g_recv.at[j, off],
            device_id={"model": partner(col, off, k)}, device_id_type=MESH)

    def backward(j, off):
        to = partner(me, off, n)
        return pltpu.make_async_remote_copy(
            src_ref=result.at[j, to], dst_ref=back_ref.at[j * n + me],
            send_sem=b_send.at[j, off], recv_sem=b_recv.at[j, off],
            device_id={"shard": to}, device_id_type=MESH)

    def mine_in(j):
        return pltpu.make_async_copy(moved.at[j, me], held.at[j, me], own_in.at[j])

    def mine_out(j):
        return pltpu.make_async_copy(result.at[j, me], back_ref.at[j * n + me], own_out.at[j])

    barrier = pltpu.get_barrier_semaphore()
    for off in range(n - 1, 0, -1):
        pl.semaphore_signal(barrier, inc=1, device_id={"shard": partner(me, off, n)}, device_id_type=MESH)
    for off in range(1, k):
        pl.semaphore_signal(barrier, inc=1, device_id={"model": partner(col, off, k)}, device_id_type=MESH)

    @pl.loop(0, local)
    def _(j):
        load_moved(j).start()
        load_grad(j).start()

    def step(j):
        load_moved(j).wait()
        load_grad(j).wait()
        moved[j] = hold_rate * moved[j] + grad[j]

    def send(j):
        for off in range(1, n):
            forward(j, off).start()
        mine_in(j).start()

    step(0)
    pl.semaphore_wait(barrier, n + k - 2)
    send(0)

    @pl.loop(1, local)
    def _(j):
        step(j)
        send(j)

    @pl.loop(0, local)
    def _(j):
        store_new(j).start()

    @pl.loop(0, local)
    def _(j):
        for off in range(1, n):
            forward(j, off).wait_recv()
        mine_in(j).wait()
        x = held[j].reshape(side, wide)
        grams[j, col] = lax.dot_general(
            x, x, (((1,), (1,)), ((), ())), precision=HIGHEST, preferred_element_type=jnp.float32)
        for off in range(1, k):
            share(j, off).start()
        for off in range(1, k):
            share(j, off).wait_recv()
        gram = grams[j, 0]
        for i in range(1, k):
            gram = gram + grams[j, i]
        result[j] = mm(direction(gram), x).reshape(n, rows, wide)
        for off in range(1, n):
            backward(j, off).start()
        mine_out(j).start()

    @pl.loop(0, local)
    def _(j):
        for off in range(1, n):
            forward(j, off).wait_send()
        for off in range(1, k):
            share(j, off).wait_send()
        store_new(j).wait()
        mine_out(j).wait()

    @pl.loop(0, local)
    def _(j):
        for off in range(1, n):
            backward(j, off).wait()


def by_kernel(n, k, gradients, momentum):
    mats, rows, wide = gradients.shape
    local = mats // n
    side = n * rows
    dma = pltpu.SemaphoreType.DMA
    whole = jax.ShapeDtypeStruct(gradients.shape, jnp.float32)
    return pl.pallas_call(
        functools.partial(exchange_kernel, n, k),
        out_shape=(whole, whole),
        in_specs=[pl.BlockSpec(memory_space=pltpu.HBM)] * 2,
        out_specs=[pl.BlockSpec(memory_space=pl.ANY)] * 2,
        scratch_shapes=[
            *[pltpu.VMEM((local, n, rows, wide), jnp.float32)] * 4,
            pltpu.VMEM((local, k, side, side), jnp.float32),
            dma((local,)), dma((local,)),
            dma((local, n)), dma((local, n)),
            dma((local, k)), dma((local, k)),
            dma((local, n)), dma((local, n)),
            dma((local,)), dma((local,)), dma((local,)),
        ],
        compiler_params=pltpu.CompilerParams(
            collective_id=0, has_side_effects=True, vmem_limit_bytes=VMEM_LIMIT),
    )(pltpu.with_memory_space_constraint(gradients, pltpu.HBM), pltpu.with_memory_space_constraint(momentum, pltpu.HBM))


def finish_kernel(pieces, back_ref, w_ref, new_ref, out_w, out_new, done, sem_w, sem_new):
    step = back_ref.shape[0] // pieces

    def part(i):
        return pl.ds(i * step, step)

    def put_new(i):
        return pltpu.make_async_copy(new_ref.at[part(i)], out_new.at[part(i)], sem_new.at[i])

    def put_w(i):
        return pltpu.make_async_copy(done.at[part(i)], out_w.at[part(i)], sem_w.at[i])

    for i in range(pieces):
        put_new(i).start()
    for i in range(pieces):
        done[part(i)] = w_ref[part(i)] - learn_rate * back_ref[part(i)]
        put_w(i).start()
    for i in range(pieces):
        put_new(i).wait()
        put_w(i).wait()


def finish(pieces, back, weights, new_momentum):
    whole = jax.ShapeDtypeStruct(back.shape, jnp.float32)
    hold = pl.BlockSpec(memory_space=pltpu.VMEM)
    leave = pl.BlockSpec(memory_space=pl.ANY)
    return pl.pallas_call(
        functools.partial(finish_kernel, pieces),
        out_shape=(whole, whole),
        in_specs=[hold, hold, leave],
        out_specs=[leave, leave],
        scratch_shapes=[
            pltpu.VMEM(back.shape, jnp.float32),
            pltpu.SemaphoreType.DMA((pieces,)), pltpu.SemaphoreType.DMA((pieces,)),
        ],
        compiler_params=pltpu.CompilerParams(vmem_limit_bytes=FINISH_LIMIT),
        cost_estimate=pl.CostEstimate(flops=2 * back.size, bytes_accessed=20 * back.size, transcendentals=0),
    )(back, weights, new_momentum)


def on_device(n, k, gradients, momentum, weights):
    back, new_momentum = by_kernel(n, k, gradients, momentum)
    return tuple(finish(n, back, weights, new_momentum))


def solution(mesh):
    placed = P(None, "shard", "model")
    return jax.shard_map(
        functools.partial(on_device, mesh.shape["shard"], mesh.shape["model"]),
        mesh=mesh,
        in_specs=(placed, placed, placed),
        out_specs=(placed, placed),
        check_vma=False,
    )
```

time: 102 us -> 100 us (0.980)
  other arithmetic: 4.71 us -> 0 us
  Pallas kernels: 96.9 us -> 99.3 us
    add x1 -> x0, other arithmetic: 2.83 us -> none  [on_device(): new_momentum = hold_rate * momentum + gradients]
    pallas_call x1 -> x2, Pallas kernels: 96.9 us -> 99.3 us  [the longest x1 97.1 us: by_kernel(): pl.pallas_call(functools.partial(exchange_kernel, n, k), out_shape=(whole...]
    sub x1 -> x0, other arithmetic: 1.88 us -> none  [on_device(): new_weights = weights - learn_rate * back]
where the time goes in v2:
time: 100 us; the launch traced here: 99.9 us
  Pallas kernels  99.3 us (99%)
    pallas_call x1, Pallas kernels, by_kernel(): pl.pallas_call(functools.partial(exchange_kernel, n, k), out_shape=(whole...  97.1 us
    pallas_call x1, Pallas kernels, finish(): pl.pallas_call(functools.partial(finish_kernel, pieces), out_shape=(whole...  2.13 us

profile of v2, /device:TPU:0, one launch (start us, length us, event | category | flops | bytes accessed | tf_op | source)
XLA Modules:
  0.0 99.9 jit_solution(14722909004781523782)
XLA Ops:
  0.6 0.0 copy-start
  0.6 97.1 %shard_map.50 = (f32[32,16,1024]{2,1,0:T(8,128)S(1)}, f32[32,16,1024]{2,1,0:T(8,128)S(1)}) custom-call(f32[32,16,1024]{2,1,0:T(8,128)} %g_ref.1, f32[32,16,1024]{2,1,0:T(8,128)} %m_ref.1), custom_call_target="tpu_custom_call" | custom-call | tf_op jit(solution)/shard_map/pallas_call | solution.py:177
  97.8 0.0 copy-done
  97.8 2.1 %shard_map.51 = (f32[32,16,1024]{2,1,0:T(8,128)}, f32[32,16,1024]{2,1,0:T(8,128)}) custom-call(f32[32,16,1024]{2,1,0:T(8,128)S(1)} %get-tuple-element.4.back_ref, f32[32,16,1024]{2,1,0:T(8,128)S(1)} %copy-done, f32[32,16,1024]{2,1,0:T(8,128)S(1)} %get-tuple-element.5.new_ref), custom_call_target="tpu_custom_call" | custom-call | flops 1048576 | bytes 10485760 | tf_op jit(solution)/shard_map/pallas_call | solution.py:222
Async XLA Ops:
  0.6 97.2 %copy-start = (f32[32,16,1024]{2,1,0:T(8,128)S(1)}, f32[32,16,1024]{2,1,0:T(8,128)}, u32[]{:S(2)}) copy-start(f32[32,16,1024]{2,1,0:T(8,128)} %w_ref.1) | copy-start | bytes 6291460
